TPU v7x, 32 devices: a whole 2x2x4 slice. The times are simulated.
32 devices in a mesh: real: 2 (over y), env: 4 (over z), mpo: 2 (over x), col: 2 (over core).
Axes of the slice: x: 2, y: 2, z: 4, core: 2. Of those that a mesh axis runs over, the one named last changes fastest.
Arguments:
- held: bfloat16 [3072, 8, 384], P(('real', 'env', 'col')), parts along dimension 0, may hold values from -0.15625 to 0.15625
- owner_map: int32 [8, 192], P('real'), parts along dimension 0, may hold values from 0 to 1535, as said below
- kept: int32 [8], P(('real', 'env')), parts along dimension 0, may hold values from 96 to 384
- left_env: bfloat16 [14, 8, 384, 384], P('mpo', ('real', 'env')), parts along dimension 1, may hold values from -6 to 6
- mpo_tensor: float32 [14, 14, 4, 4], replicated, may hold values from -1 to 1
- mpo_mask: int32 [14, 14], replicated, may hold values 0 or 1
- fields: float32 [4], P('real'), parts along dimension 0, may hold values from -2 to 2
Outputs:
- new_env: float32 [14, 8, 384, 384], P('mpo', ('real', 'env'), None, 'col'), parts along dimension 1
There are 2 independent parts, one for each index of `real`. A program takes and returns all parts, laid end to end along the dimension named above; an argument that names none is the same for every part. Nothing has to cross between parts.
Inputs may be any that keep to these rules, and one draw needn't show every extreme that they name: owner_map[t, j] is the slot of held that holds tile j of sector t; all entries differ. The owner of index o along env+col holds the slots o * 192 to (o + 1) * 192 - 1. Among the tiles of one sector (the sector of one env index), one owner holds at most 48, and for every sector some owner holds exactly 48.
All inputs are finite; a program needn't handle non-finite values.
Results may differ from a plain program's by a relative error of at most 0.0042.
Values may be sent and summed in bfloat16 or wider, within the bound.
A program may use at most 64 MiB of HBM per device.

v0:
```python
import jax
import jax.numpy as jnp
from jax import lax
from jax.sharding import PartitionSpec as P


def build_couplings(mpo_tensor, mpo_mask, fields, padded):
    bond = mpo_tensor.shape[0]
    states = mpo_tensor.shape[2]
    base = mpo_tensor * mpo_mask.astype(jnp.float32)[:, :, None, None]
    level = jnp.arange(states, dtype=jnp.int32)
    spin_first = 0.5 - (level // 2).astype(jnp.float32)
    spin_second = 0.5 - (level % 2).astype(jnp.float32)
    onsite = jnp.diag(fields[0] * spin_first + fields[1] * spin_second)
    bond_index = jnp.arange(bond, dtype=jnp.int32)
    corner = (bond_index[:, None] == bond - 1) & (bond_index[None, :] == 0)
    base = base + jnp.where(corner[:, :, None, None], onsite[None, None, :, :], jnp.float32(0.0))
    return jnp.pad(base, ((0, padded - bond), (0, padded - bond), (0, 0), (0, 0)))


def on_device(held, owner_map, kept, left_env, mpo_tensor, mpo_mask, fields):
    env_count = lax.axis_size("env")
    core_count = lax.axis_size("col")
    plane_count = lax.axis_size("mpo")
    env_row = lax.axis_index("env")
    core = lax.axis_index("col")
    plane = lax.axis_index("mpo")
    pool, tile, width = held.shape
    sectors_here = kept.shape[0]
    tiles_sector = owner_map.shape[1]
    states = tiles_sector * tile // width
    per_row = sectors_here * tiles_sector
    capacity = 2 * per_row // (env_count * core_count)
    owner_self = env_row * core_count + core
    leading_sector = lax.Precision.HIGHEST
    holder = owner_map // pool
    local_slot = owner_map % pool
    mine = (holder == owner_self).astype(jnp.int32)
    rank = jnp.cumsum(mine, axis=1) - 1
    slot_ids = jnp.arange(capacity, dtype=jnp.int32)
    picked = (mine[:, None, :] == 1) & (rank[:, None, :] == slot_ids[None, :, None])
    source_slot = jnp.sum(jnp.where(picked, local_slot[:, None, :], 0), axis=2)
    outgoing = jnp.take(held, source_slot.reshape(-1), axis=0).reshape(
        env_count, capacity, tile, width
    )
    arrived = lax.all_to_all(outgoing, "env", split_axis=0, concat_axis=0, tiled=True)
    arrived = lax.all_gather(arrived, "col", axis=1, tiled=True)
    mine_rows = lax.dynamic_slice_in_dim(
        owner_map, env_row * sectors_here, sectors_here, 0
    ).reshape(per_row)
    sender = mine_rows // pool
    position = jnp.arange(per_row, dtype=jnp.int32)
    earlier = (sender[:, None] == sender[None, :]) & (position[None, :] < position[:, None])
    order_within = jnp.sum(earlier.astype(jnp.int32), axis=1)
    index = (
        sender // core_count * (core_count * capacity)
        + sender % core_count * capacity
        + order_within
    )
    flat = arrived.reshape(env_count * core_count * capacity, tile * width)
    sector_matrices = jnp.take(flat, index, axis=0).reshape(sectors_here, states, width, width)
    columns = jnp.arange(width, dtype=jnp.int32)
    keep = columns[None, :] < kept[:, None]
    sector_matrices = jnp.where(
        keep[:, None, None, :], sector_matrices, jnp.zeros((), jnp.bfloat16)
    )
    slab = left_env.shape[0]
    couplings = build_couplings(mpo_tensor, mpo_mask, fields, slab * plane_count)
    share = width // core_count
    own_columns = lax.dynamic_slice_in_dim(sector_matrices, core * share, share, 3)
    mine_coupling = lax.dynamic_slice_in_dim(couplings, plane * slab, slab, 0)
    firsts = jnp.einsum(
        "wij,sja->wsia", left_env[:, 0], own_columns[0], preferred_element_type=jnp.float32
    )
    next_spin = jnp.einsum(
        "wvts,wsia->vtia", mine_coupling, firsts, precision=leading_sector
    ).astype(jnp.bfloat16)
    operator_pieces = [
        jnp.einsum(
            "hze,shzo->seo", sector_matrices[0], next_spin, preferred_element_type=jnp.float32
        )
    ]
    return lax.psum_scatter(
        jnp.stack(operator_pieces, axis=1), "mpo", scatter_dimension=0, tiled=True
    )


def solution(mesh):
    return jax.shard_map(
        on_device,
        mesh=mesh,
        in_specs=(
            P(("real", "env", "col"), None, None),
            P("real", None),
            P(("real", "env")),
            P("mpo", ("real", "env"), None, None),
            P(),
            P(),
            P("real"),
        ),
        out_specs=P("mpo", ("real", "env"), None, "col"),
        check_vma=False,
    )
```

profile of v0, /device:TPU:0, one launch (start us, length us, event | category | flops | bytes accessed | tf_op | source)
XLA Modules:
  0.0 178.0 jit_solution(5133572742111971022)
XLA Ops:
  6.5 0.8 add_select_fusion
  7.4 0.7 fusion.61
  8.1 0.1 and.160
  8.2 0.5 broadcast.503
  8.7 1.4 fusion.60
  10.1 0.1 div.57
  10.2 0.2 convert_reduce_fusion
  10.4 0.1 reduce_sum.23
  10.4 0.7 broadcast_compare_fusion
  11.2 1.2 reduce-window.6
  12.5 0.1 copy.15
  12.6 0.1 copy.16
  12.8 0.2 select_reduce_fusion
  13.0 0.1 reshape.354
  13.1 2.2 %gather_fusion = bf16[192,8,384]{2,1,0:T(8,128)(2,1)S(1)} fusion(bf16[192,8,384]{2,1,0:T(8,128)(2,1)} %param.7, s32[1024]{0:T(1024)S(1)} %pad_clamp_fusion.1), kind=kCustom, calls=%fused_computation | custom fusion | bytes 2360064 | tf_op jit(solution)/shard_map/jit(_take)/gather | solution.py:43
  15.4 0.3 broadcast_select_fusion
  15.7 34.8 %all_to_all.5 = bf16[4,48,8,384]{3,2,1,0:T(8,128)(2,1)} all-to-all(bf16[4,48,8,384]{3,2,1,0:T(8,128)(2,1)S(1)} %broadcast_select_fusion), channel_id=1, replica_groups=mesh['real'=2,'env'=4,'mpo'=2,'col'=2] {'env'}, dimensions={0} | all-to-all | bytes 2359296 | tf_op jit(solution)/shard_map/all_to_all | solution.py:46
  51.2 0.1 broadcast_in_dim.116
  51.3 0.1 broadcast_in_dim.117
  51.5 0.6 fusion.63
  52.1 1.2 fusion.51
  53.6 7.1 %all-gather.2.cloned.1.call-done = bf16[4,96,8,384]{3,2,1,0:T(8,128)(2,1)} async-done(((bf16[4,48,8,384]{3,2,1,0:T(8,128)(2,1)}), bf16[4,96,8,384]{3,2,1,0:T(8,128)(2,1)}) %all-gather.2.cloned.1.call-update) | async-done | bytes 2359312 | tf_op jit(solution)/shard_map/all_gather | solution.py:47
  60.7 3.6 %copy.28 = bf16[48,8,8,384]{3,1,2,0:T(8,128)(2,1)} copy(bf16[48,8,8,384]{3,2,1,0:T(8,128)(2,1)} %bitcast.75) | data formatting | bytes 4718592
  64.3 4.5 %gather_fusion.1 = bf16[192,3072]{1,0:T(8,128)(2,1)S(1)} fusion(bf16[384,3072]{1,0:T(8,128)(2,1)} %bitcast.73, s32[1024]{0:T(1024)S(1)} %pad_clamp_fusion), kind=kCustom, calls=%fused_computation.1 | custom fusion | bytes 2360064 | tf_op jit(solution)/shard_map/jit(_take)/gather | solution.py:61
  68.7 1.4 gather.17
  70.1 1.4 gather.18
  71.5 1.6 constant_dynamic-slice_fusion.2
  73.1 0.3 copy.26
  73.4 2.4 %convolution_bitcast_fusion = f32[7,4,384,192]{2,3,0,1:T(8,128)S(1)} fusion(bf16[7,1,384,384]{3,2,1,0:T(8,128)(2,1)S(1)} %copy-done, bf16[1,4,384,192]{2,3,1,0:T(8,128)(2,1)S(1)} %copy.26, pred[192]{0:T(512)(128)(4,1)S(1)} %dynamic-slice.2, pred[4,384]{1,0:T(4,128)(4,1)S(1)} %broadcast_in_dim.117), kind=kOutput, calls=%fused_computation.8 | convolution fusion | flops 1586036736 | bytes 10913472 | tf_op jit(solution)/shard_map/wij,sja->wsia/dot_general | solution.py:72
  75.9 33.6 %bitcast_convert_fusion = bf16[14,4,384,192]{2,0,3,1:T(8,128)(2,1)S(1)} fusion(f32[7,4,384,192]{2,3,0,1:T(8,128)S(1)} %convolution_bitcast_fusion, f32[7,14,4,4,1]{1,3,0,4,2:T(4,128)S(1)} %fusion.67), kind=kOutput, calls=%fused_computation.2 | convolution fusion | flops 1391394816 | bytes 16521344 | tf_op jit(solution)/shard_map/wvts,wsia->vtia/dot_general | solution.py:75
  109.5 6.7 %fusion.7 = f32[14,1,384,192]{2,3,0,1:T(8,128)} fusion(bf16[14,4,384,192]{2,0,3,1:T(8,128)(2,1)S(1)} %bitcast_convert_fusion, bf16[4,384,384]{2,1,0:T(8,128)(2,1)S(1)} %copy-done.1, pred[4,384]{1,0:T(4,128)(4,1)S(1)} %broadcast_in_dim.117, pred[384]{0:T(512)(128)(4,1)S(1)} %iota_compare_fusion.2), kind=kOutput, calls=%fused_computation.9 | convolution fusion | flops 3172073472 | bytes 13567872 | tf_op jit(solution)/shard_map/hze,shzo->seo/dot_general | solution.py:79
  116.2 55.0 %reduce-scatter.2.cloned.1.call-done = f32[7,1,384,192]{2,3,0,1:T(8,128)} async-done(((f32[14,1,384,192]{2,3,0,1:T(8,128)}), f32[7,1,384,192]{2,3,0,1:T(8,128)}) %reduce-scatter.2.cloned.1.call-update) | async-done | bytes 2064400 | tf_op jit(solution)/shard_map/reduce_scatter | solution.py:83
  (37 shorter events, 0.7 us)
Async XLA Ops:
  6.5 66.9 %copy-start = (bf16[7,1,384,384]{3,2,1,0:T(8,128)(2,1)S(1)}, bf16[7,1,384,384]{3,2,1,0:T(8,128)(2,1)}, u32[]{:S(2)}) copy-start(bf16[7,1,384,384]{3,2,1,0:T(8,128)(2,1)} %param.10) | copy-start | bytes 6193156
  6.5 54.2 %all-gather.2.cloned.1.call-start = ((), (), s32[]{:S(2)}) async-start(), calls=%async_computation.2 | async-start | bytes 3538944 | tf_op jit(solution)/shard_map/all_gather | solution.py:47
  50.4 0.8 copy-start.3
  50.4 1.1 copy-start.4
  50.4 3.1 %copy-start.2 = (f32[14,14,4,4]{1,3,2,0:T(4,128)S(1)}, f32[14,14,4,4]{1,3,2,0:T(4,128)}, u32[]{:S(2)}) copy-start(f32[14,14,4,4]{1,3,2,0:T(4,128)} %param.11) | copy-start | bytes 37636
  50.5 120.7 %reduce-scatter.2.cloned.1.call-start = ((), (), s32[]{:S(2)}) async-start(), calls=%async_computation.3 | async-start | bytes 6193152 | tf_op jit(solution)/shard_map/reduce_scatter | solution.py:83
  75.9 33.6 %copy-start.1 = (bf16[4,384,384]{2,1,0:T(8,128)(2,1)S(1)}, bf16[4,384,384]{2,1,0:T(8,128)(2,1)}, u32[]{:S(2)}) copy-start(bf16[4,384,384]{2,1,0:T(8,128)(2,1)} %gather.18) | copy-start | bytes 3538948
Sparse Core Ops, SparseCore 0:
  50.6 10.0 all-gather.1
  116.3 54.8 reduce-scatter.1
where the time goes:
time: 178 us
  waiting for transfers between devices  62.1 us (35%)
  matrix products  42.7 us (24%)
  blocking collectives  34.8 us (20%)
  local copies, waits for them, and re-layouts  17 us (10%)
  between operations  14.3 us (8%)
  other arithmetic  7.13 us (4%)
    reduce_scatter x1, waiting for transfers between devices, on_device(): lax.psum_scatter(jnp.stack(operator_pieces, axis=1), 'mpo', scatter_dimen...  55 us
    all_to_all x1, blocking collectives, on_device(): lax.all_to_all(outgoing, 'env', split_axis=0, concat_axis=0, tiled=True)  34.8 us
    dot_general x1, matrix products, on_device(): jnp.einsum('wvts,wsia->vtia', mine_coupling, firsts, precision=leading_se...  33.6 us
    gather x3, local copies, waits for them, and re-layouts, on_device(): jnp.take(flat, index, axis=0).reshape(sectors_here, states, width, width)  7.22 us
    all_gather x1, waiting for transfers between devices, on_device(): arrived = lax.all_gather(arrived, 'col', axis=1, tiled=True)  7.07 us
    dot_general x1, matrix products, on_device(): jnp.einsum('hze,shzo->seo', sector_matrices[0], next_spin, preferred_elem...  6.67 us
    unnamed x13, local copies, waits for them, and re-layouts  3.93 us
  transfers between devices with their start and end apart: 2, of which 2 were waited for; matrix products, arithmetic and copies ran while one was open for 1% of the time, Pallas kernels for 0%

commit v1 on v0

v1 whole, which is shorter than its diff:
```python
import functools

import jax
import jax.numpy as jnp
from jax import lax
from jax.experimental import pallas as pl
from jax.experimental.pallas import tpu as pltpu
from jax.sharding import PartitionSpec as P

MESH = pl.DeviceIdType.MESH
LANES = 128
GROUP = 4
BF = jnp.bfloat16


def build_couplings(mpo_tensor, mpo_mask, fields, padded):
    bond = mpo_tensor.shape[0]
    states = mpo_tensor.shape[2]
    base = mpo_tensor * mpo_mask.astype(jnp.float32)[:, :, None, None]
    level = jnp.arange(states, dtype=jnp.int32)
    spin_first = 0.5 - (level // 2).astype(jnp.float32)
    spin_second = 0.5 - (level % 2).astype(jnp.float32)
    onsite = jnp.diag(fields[0] * spin_first + fields[1] * spin_second)
    bond_index = jnp.arange(bond, dtype=jnp.int32)
    corner = (bond_index[:, None] == bond - 1) & (bond_index[None, :] == 0)
    base = base + jnp.where(corner[:, :, None, None], onsite[None, None, :, :], jnp.float32(0.0))
    return jnp.pad(base, ((0, padded - bond), (0, padded - bond), (0, 0), (0, 0)))


def iota(shape, dim):
    return lax.broadcasted_iota(jnp.int32, shape, dim)


def one_hot(condition):
    return jnp.where(condition, jnp.float32(1), jnp.float32(0)).astype(BF)


def mm(a, b):
    return jnp.dot(a, b, preferred_element_type=jnp.float32)


def pack_kernel(cores, map_ref, held_ref, out_ref):
    pool = held_ref.shape[0]
    rows, tiles = map_ref.shape
    low = (lax.axis_index("env") * cores + lax.axis_index("col")) * pool

    def sector(t, carry):
        def step(j, count):
            slot = map_ref[t, j] - low
            mine = (slot >= 0) & (slot < pool)
            out_ref[t, count] = held_ref[jnp.where(mine, slot, 0)]
            return count + mine.astype(jnp.int32)

        lax.fori_loop(0, tiles, step, jnp.int32(0), unroll=8)
        return carry

    lax.fori_loop(0, rows, sector, jnp.int32(0))


def comm_kernel(
    sizes, pack_ref, left_ref, arrived_ref, other_ref,
    z_send, z_recv, f_send, f_recv, x_send, x_recv, g_send, g_recv, own_sem,
):
    envs, planes, cores = sizes
    env, plane, core = lax.axis_index("env"), lax.axis_index("mpo"), lax.axis_index("col")
    cap = arrived_ref.shape[1]
    slab = left_ref.shape[0]
    part = left_ref.shape[2] // cores
    mate = lax.rem(core + 1, cores)

    barrier = pltpu.get_barrier_semaphore()
    for d in range(1, envs):
        pl.semaphore_signal(
            barrier, inc=1, device_id={"env": lax.rem(env + d, envs)}, device_id_type=MESH
        )
    for d in range(1, planes):
        pl.semaphore_signal(
            barrier, inc=1, device_id={"mpo": lax.rem(plane + d, planes)}, device_id_type=MESH
        )
    pl.semaphore_signal(barrier, inc=1, device_id={"col": mate}, device_id_type=MESH)
    pl.semaphore_wait(barrier, envs + planes - 1)

    def z_copy(d):
        target = lax.rem(env + d, envs)
        return pltpu.make_async_remote_copy(
            src_ref=pack_ref.at[target, pl.ds(0, cap)],
            dst_ref=arrived_ref.at[env * cores + core],
            send_sem=z_send.at[d], recv_sem=z_recv.at[d],
            device_id={"env": target}, device_id_type=MESH,
        )

    def f_copy(d):
        source = lax.rem(env - d + envs, envs)
        block = arrived_ref.at[source * cores + core]
        return pltpu.make_async_remote_copy(
            src_ref=pack_ref.at[env, pl.ds(0, cap)] if d == 0 else block,
            dst_ref=block,
            send_sem=f_send.at[d], recv_sem=f_recv.at[d],
            device_id={"col": mate}, device_id_type=MESH,
        )

    def x_copy(d, w):
        rows = pl.ds(pl.multiple_of(core * part, part), part)
        return pltpu.make_async_remote_copy(
            src_ref=left_ref.at[w, 0, rows],
            dst_ref=other_ref.at[(planes - d - 1) * slab + w, rows],
            send_sem=x_send.at[d, w], recv_sem=x_recv.at[d, w],
            device_id={"mpo": lax.rem(plane + d, planes)}, device_id_type=MESH,
        )

    def g_copy(d, w):
        rows = pl.ds(pl.multiple_of(core * part, part), part)
        piece = other_ref.at[(planes - d - 1) * slab + w, rows]
        return pltpu.make_async_remote_copy(
            src_ref=piece, dst_ref=piece,
            send_sem=g_send.at[d, w], recv_sem=g_recv.at[d, w],
            device_id={"col": mate}, device_id_type=MESH,
        )

    own = pltpu.make_async_copy(
        pack_ref.at[env, pl.ds(0, cap)], arrived_ref.at[env * cores + core], own_sem
    )
    z_order = list(range(envs - 1, 0, -1))
    x_order = [(d, w) for w in range(slab) for d in range(1, planes)]
    for d in z_order:
        z_copy(d).start()
    for d, w in x_order:
        x_copy(d, w).start()
    own.start()
    f_copy(0).start()

    waits = [("z", d, (i + 1) / len(z_order)) for i, d in enumerate(z_order)]
    waits += [("x", item, (i + 1) / len(x_order)) for i, item in enumerate(x_order)]
    for kind, item, _ in sorted(waits, key=lambda entry: entry[2]):
        if kind == "z":
            z_copy(item).wait_recv()
            f_copy(item).start()
        else:
            x_copy(*item).wait_recv()
            g_copy(*item).start()
    own.wait()
    f_copy(0).wait()
    for d in z_order:
        z_copy(d).wait_send()
        f_copy(d).wait()
    for item in x_order:
        x_copy(*item).wait_send()
        g_copy(*item).wait()


def contract_kernel(
    cores, pool, map_ref, kept_ref, arrived_ref, left_ref, other_ref, coupling_ref,
    out_ref, count_ref, tiles_ref, own_ref, turned_ref, first_ref, second_ref,
):
    env, core = lax.axis_index("env"), lax.axis_index("col")
    owners, cap, tile, width = arrived_ref.shape
    tiles = map_ref.shape[1]
    states = tiles * tile // width
    slab = left_ref.shape[0]
    slots = slab + other_ref.shape[0]
    padded = coupling_ref.shape[1] // states
    share = width // cores
    lanes = own_ref.shape[2]

    for s in range(owners):
        count_ref[s] = 0

    def fetch(j, carry):
        source = lax.div(map_ref[env, j], jnp.int32(pool))
        rank = count_ref[source]
        count_ref[source] = rank + 1
        tiles_ref[pl.ds(pl.multiple_of(j * tile, tile), tile), :] = arrived_ref[
            source, rank
        ].astype(jnp.float32)
        return carry

    lax.fori_loop(0, tiles, fetch, jnp.int32(0), unroll=8)

    kept = kept_ref[0]
    blocks = [
        jnp.where(
            iota((width, width), 1) < kept, tiles_ref[pl.ds(s * width, width), :], 0.0
        ).astype(BF)
        for s in range(states)
    ]

    pick = one_hot(
        (iota((width, lanes), 0) == iota((width, lanes), 1) + core * share)
        & (iota((width, lanes), 1) < share)
    )
    for s in range(states):
        own_ref[s] = mm(blocks[s], pick).astype(BF)

    chunk = 256 // states
    span = chunk * states
    row, col = iota((span, span), 0), iota((span, span), 1)
    unit = states * GROUP
    moved = (
        lax.rem(lax.div(row, GROUP), states) * chunk
        + lax.div(row, unit) * GROUP
        + lax.rem(row, GROUP)
    )
    regroup = one_hot(col == moved)
    for h in range(width // chunk):
        stack = jnp.concatenate(
            [blocks[s][h * chunk : (h + 1) * chunk] for s in range(states)], axis=0
        )
        turned_ref[:, pl.ds(h * span, span)] = mm(regroup, stack).T.astype(BF)

    pairs = slab * states
    tall, wide = pairs * GROUP, states * GROUP * padded
    spread_rows = one_hot(lax.div(iota((tall, pairs), 0), GROUP) == iota((tall, pairs), 1))
    source, target = iota((states * padded, wide), 0), iota((states * padded, wide), 1)
    spread_columns = one_hot(
        (lax.div(source, padded) == lax.div(target, GROUP * padded))
        & (lax.rem(source, padded) == lax.rem(target, padded))
    )
    diagonal = lax.rem(iota((tall, wide), 0), GROUP) == lax.rem(
        lax.div(iota((tall, wide), 1), padded), GROUP
    )
    coupling = coupling_ref[...]
    high = coupling.astype(BF)
    low = (coupling - high.astype(jnp.float32)).astype(BF)
    both = []
    for piece in (high, low):
        spread = mm(mm(spread_rows, piece).astype(BF), spread_columns)
        both.append(jnp.where(diagonal, spread, 0.0).astype(BF))
    mixing = jnp.concatenate(both, axis=0)

    step = 16
    block_rows = step * padded
    row, col = iota((block_rows, block_rows), 0), iota((block_rows, block_rows), 1)
    interleave = one_hot(col == lax.rem(row, padded) * step + lax.div(row, padded))
    rows_chunk = first_ref.shape[1] // padded
    per_group = GROUP * padded

    def chunk_step(h, carry):
        pieces = []
        for b in range(rows_chunk // step):
            rows = pl.ds(pl.multiple_of(h * rows_chunk + b * step, step), step)
            stack = [left_ref[w, 0, rows, :] for w in range(slab)]
            stack += [other_ref[w, rows, :] for w in range(slots - slab)]
            if padded > slots:
                stack.append(jnp.zeros(((padded - slots) * step, width), BF))
            pieces.append(mm(interleave, jnp.concatenate(stack, axis=0)).astype(BF))
        environment = jnp.concatenate(pieces, axis=0)
        for s in range(states):
            first_ref[s] = mm(environment, own_ref[s]).astype(BF)
        for g in range(rows_chunk // GROUP):
            operand = jnp.concatenate(
                [first_ref[s, pl.ds(g * per_group, per_group), :] for s in range(states)], axis=0
            )
            mixed = mm(mixing, operand)
            mixed = (mixed[:tall] + mixed[tall:]).astype(BF)
            at = pl.multiple_of(h * (rows_chunk * states) + g * unit, unit)
            for v in range(slab):
                second_ref[v, pl.ds(at, unit), :] = mixed[v * unit : (v + 1) * unit]
        return carry

    lax.fori_loop(0, width // rows_chunk, chunk_step, jnp.int32(0))

    def close(v, carry):
        out_ref[v] = mm(turned_ref[...], second_ref[v]).T[:share]
        return carry

    lax.fori_loop(0, slab, close, jnp.int32(0))


def on_device(held, owner_map, kept, left_env, mpo_tensor, mpo_mask, fields):
    envs, cores, planes = (lax.axis_size(name) for name in ("env", "col", "mpo"))
    plane = lax.axis_index("mpo")
    pool, tile, width = held.shape
    rows, tiles = owner_map.shape
    states = tiles * tile // width
    cap = 2 * kept.shape[0] * tiles // (envs * cores)
    slab = left_env.shape[0]
    slots = slab * planes
    padded = -(-slots // 16) * 16
    share = width // cores
    lanes = -(-share // LANES) * LANES
    smem = pl.BlockSpec(memory_space=pltpu.SMEM)
    vmem = pl.BlockSpec(memory_space=pltpu.VMEM)
    anywhere = pl.BlockSpec(memory_space=pl.ANY)
    dma = pltpu.SemaphoreType.DMA

    packed = pl.pallas_call(
        functools.partial(pack_kernel, cores),
        out_shape=jax.ShapeDtypeStruct((rows, cap + 1, tile, width), BF),
        in_specs=[smem, vmem],
        out_specs=vmem,
        name="pack",
    )(owner_map, held)

    arrived, other = pl.pallas_call(
        functools.partial(comm_kernel, (envs, planes, cores)),
        out_shape=[
            jax.ShapeDtypeStruct((envs * cores, cap, tile, width), BF),
            jax.ShapeDtypeStruct((slots - slab, width, width), BF),
        ],
        in_specs=[anywhere, anywhere],
        out_specs=[anywhere, anywhere],
        scratch_shapes=[
            dma((envs,)), dma((envs,)), dma((envs,)), dma((envs,)),
            dma((planes, slab)), dma((planes, slab)), dma((planes, slab)), dma((planes, slab)),
            dma,
        ],
        compiler_params=pltpu.CompilerParams(collective_id=0, has_side_effects=True),
        name="exchange",
    )(packed, left_env)

    couplings = build_couplings(mpo_tensor, mpo_mask, fields, slots)
    couplings = lax.dynamic_slice_in_dim(couplings, plane * slab, slab, 1)
    couplings = jnp.concatenate([couplings, couplings], axis=0)
    couplings = lax.dynamic_slice_in_dim(couplings, plane * slab, slots, 0)
    couplings = jnp.pad(couplings, ((0, padded - slots), (0, 0), (0, 0), (0, 0)))
    couplings = couplings.transpose(1, 2, 3, 0).reshape(slab * states, states * padded)

    chunk_rows = 64 * padded
    result = pl.pallas_call(
        functools.partial(contract_kernel, cores, pool),
        out_shape=jax.ShapeDtypeStruct((slab, share, width), jnp.float32),
        in_specs=[smem, smem, vmem, vmem, vmem, vmem],
        out_specs=vmem,
        scratch_shapes=[
            pltpu.SMEM((envs * cores,), jnp.int32),
            pltpu.VMEM((tiles * tile, width), jnp.float32),
            pltpu.VMEM((states, width, lanes), BF),
            pltpu.VMEM((width, tiles * tile), BF),
            pltpu.VMEM((states, chunk_rows, lanes), BF),
            pltpu.VMEM((slab, tiles * tile, lanes), BF),
        ],
        compiler_params=pltpu.CompilerParams(vmem_limit_bytes=48 * 1024 * 1024),
        name="contract",
    )(owner_map, kept, arrived, left_env, other, couplings)
    return jnp.swapaxes(result, 1, 2)[:, None]


def solution(mesh):
    return jax.shard_map(
        on_device,
        mesh=mesh,
        in_specs=(
            P(("real", "env", "col"), None, None),
            P("real", None),
            P(("real", "env")),
            P("mpo", ("real", "env"), None, None),
            P(),
            P(),
            P("real"),
        ),
        out_specs=P("mpo", ("real", "env"), None, "col"),
        check_vma=False,
    )
```

time: 178 us -> 71.5 us (0.40)
  Pallas kernels: 0 us -> 64.4 us
  waiting for transfers between devices: 62.1 us -> 0 us
  matrix products: 42.7 us -> 0 us
  blocking collectives: 34.8 us -> 0 us
  between operations: 14.3 us -> 0.76 us
  local copies, waits for them, and re-layouts: 17 us -> 3.54 us
  other arithmetic: 7.13 us -> 2.41 us
    pallas_call x0 -> x3, Pallas kernels: none -> 64.4 us  [the longest x1 34.9 us: on_device(): pl.pallas_call(functools.partial(comm_kernel, (envs, planes, cores)), out...]
    reduce_scatter x1 -> x0, waiting for transfers between devices: 55 us -> none  [on_device(): lax.psum_scatter(jnp.stack(operator_pieces, axis=1), 'mpo', scatter_dimen...]
    dot_general x3 -> x0, matrix products: 42.7 us -> none  [the longest x1 33.6 us: on_device(): jnp.einsum('wvts,wsia->vtia', mine_coupling, firsts, precision=leading_se...]
    all_to_all x1 -> x0, blocking collectives: 34.8 us -> none  [on_device(): lax.all_to_all(outgoing, 'env', split_axis=0, concat_axis=0, tiled=True)]
    gather x4 -> x0, local copies, waits for them, and re-layouts: 9.45 us -> none  [the longest x3 7.22 us: on_device(): jnp.take(flat, index, axis=0).reshape(sectors_here, states, width, width)]
    all_gather x1 -> x0, waiting for transfers between devices: 7.07 us -> none  [on_device(): arrived = lax.all_gather(arrived, 'col', axis=1, tiled=True)]
    unnamed x13 -> x9, local copies, waits for them, and re-layouts: 3.93 us -> 1.81 us
  transfers between devices with their start and end apart: 2 -> 0, of which waited for: 2 -> 0; matrix products, arithmetic and copies ran while one was open for 1% -> 0% of each run, Pallas kernels for 0% -> 0%
where the time goes in v1:
time: 71.5 us; the launch traced here: 71.2 us
  Pallas kernels  64.4 us (90%)
  local copies, waits for them, and re-layouts  3.54 us (5%)
  other arithmetic  2.41 us (3%)
  between operations  0.76 us (1%)
    pallas_call x1, Pallas kernels, on_device(): pl.pallas_call(functools.partial(comm_kernel, (envs, planes, cores)), out...  34.9 us
    pallas_call x1, Pallas kernels, on_device(): pl.pallas_call(functools.partial(contract_kernel, cores, pool), out_shape...  21.7 us
    pallas_call x1, Pallas kernels, on_device(): pl.pallas_call(functools.partial(pack_kernel, cores), out_shape=jax.Shape...  7.9 us
    unnamed x9, local copies, waits for them, and re-layouts  1.81 us

profile of v1, /device:TPU:0, one launch (start us, length us, event | category | flops | bytes accessed | tf_op | source)
XLA Modules:
  0.0 71.2 jit_solution(6771763010461190376)
XLA Ops:
  0.0 0.0 copy-start
  0.7 1.4 %fusion.8 = (f32[1]{0:T(128)}, f32[1]{0:T(128)}) fusion(f32[2]{0:T(128)} %param.13), kind=kLoop, calls=%fused_computation.23 | loop fusion | bytes 16 | tf_op jit(solution)/shard_map/slice | solution.py:23
  2.1 1.3 %fusion.4 = f32[4]{0:T(128)S(1)} fusion(f32[]{:T(128)} %bitcast.1, f32[]{:T(128)} %bitcast), kind=kLoop, calls=%fused_computation.17 | loop fusion | flops 76 | bytes 24 | tf_op jit(solution)/shard_map/add | solution.py:23
  3.4 0.1 broadcast_and_fusion
  3.5 0.1 fusion
  3.6 0.7 convert_element_type.19
  4.3 0.1 copy.10
  4.4 0.0 copy-done
  4.4 0.1 constant_dynamic-slice_fusion.1
  4.5 0.2 copy.13
  4.8 0.1 select_add_fusion
  4.8 0.1 dynamic-slice_maximum_fusion
  5.0 0.1 reshape.88.coupling_ref
  5.1 7.9 %pack.1.pack_ref = bf16[4,49,8,384]{3,2,1,0:T(8,128)(2,1)} custom-call(s32[4,192]{1,0:T(4,128)} %map_ref.3, bf16[192,8,384]{2,1,0:T(8,128)(2,1)} %held_ref.1), custom_call_target="tpu_custom_call" | custom-call | tf_op jit(solution)/shard_map/pack/pallas_call | solution.py:286
  13.0 0.0 copy-start.1
  13.0 0.0 copy-start.3
  13.0 34.9 %exchange.1 = (bf16[8,48,8,384]{3,2,1,0:T(8,128)(2,1)}, bf16[7,384,384]{2,1,0:T(8,128)(2,1)}) custom-call(bf16[4,49,8,384]{3,2,1,0:T(8,128)(2,1)} %pack.1.pack_ref, bf16[7,1,384,384]{3,2,1,0:T(8,128)(2,1)} %left_ref.3), custom_call_target="tpu_custom_call" | custom-call | tf_op jit(solution)/shard_map/exchange/pallas_call | solution.py:294
  47.9 0.0 copy-done.1
  47.9 0.0 copy-done.3
  47.9 0.0 copy-start.2
  47.9 1.6 %copy-done.2 = bf16[7,384,384]{2,1,0:T(8,128)(2,1)S(1)} copy-done((bf16[7,384,384]{2,1,0:T(8,128)(2,1)S(1)}, bf16[7,384,384]{2,1,0:T(8,128)(2,1)}, u32[]{:S(2)}) %copy-start.2) | copy-done | bytes 2064408
  49.5 21.7 %contract.1 = f32[7,192,384]{2,1,0:T(8,128)} custom-call(s32[4,192]{1,0:T(4,128)S(1)} %copy-done.3, s32[1]{0:T(128)S(6)} %copy.14.kept_ref, bf16[8,48,8,384]{3,2,1,0:T(8,128)(2,1)} %get-tuple-element.7.arrived_ref, bf16[7,1,384,384]{3,2,1,0:T(8,128)(2,1)S(1)} %copy-done.1, bf16[7,384,384]{2,1,0:T(8,128)(2,1)S(1)} %copy-done.2, f32[28,64]{1,0:T(8,128)S(1)} %reshape.88.coupling_ref), custom_call_target="tpu_custom_call" | custom-call | tf_op jit(solution)/shard_map/contract/pallas_call | solution.py:319
  (4 shorter events, 0.0 us)
Async XLA Ops:
  0.0 4.4 %copy-start = (f32[14,14,4,4]{1,3,2,0:T(4,128)S(1)}, f32[14,14,4,4]{1,3,2,0:T(4,128)}, u32[]{:S(2)}) copy-start(f32[14,14,4,4]{1,3,2,0:T(4,128)} %param.11) | copy-start | bytes 37636
  13.0 34.9 %copy-start.1 = (bf16[7,1,384,384]{3,2,1,0:T(8,128)(2,1)S(1)}, bf16[7,1,384,384]{3,2,1,0:T(8,128)(2,1)}, u32[]{:S(2)}) copy-start(bf16[7,1,384,384]{3,2,1,0:T(8,128)(2,1)} %left_ref.3) | copy-start | bytes 6193156
  13.0 34.9 %copy-start.3 = (s32[4,192]{1,0:T(4,128)S(1)}, s32[4,192]{1,0:T(4,128)}, u32[]{:S(2)}) copy-start(s32[4,192]{1,0:T(4,128)} %map_ref.3) | copy-start | bytes 9220
  47.9 1.6 %copy-start.2 = (bf16[7,384,384]{2,1,0:T(8,128)(2,1)S(1)}, bf16[7,384,384]{2,1,0:T(8,128)(2,1)}, u32[]{:S(2)}) copy-start(bf16[7,384,384]{2,1,0:T(8,128)(2,1)} %get-tuple-element.8.other_ref) | copy-start | bytes 6193156

commit v2 on v1

--- a/solution.py
+++ b/solution.py
@@ -13,20 +13,6 @@
 BF = jnp.bfloat16
 
 
-def build_couplings(mpo_tensor, mpo_mask, fields, padded):
-    bond = mpo_tensor.shape[0]
-    states = mpo_tensor.shape[2]
-    base = mpo_tensor * mpo_mask.astype(jnp.float32)[:, :, None, None]
-    level = jnp.arange(states, dtype=jnp.int32)
-    spin_first = 0.5 - (level // 2).astype(jnp.float32)
-    spin_second = 0.5 - (level % 2).astype(jnp.float32)
-    onsite = jnp.diag(fields[0] * spin_first + fields[1] * spin_second)
-    bond_index = jnp.arange(bond, dtype=jnp.int32)
-    corner = (bond_index[:, None] == bond - 1) & (bond_index[None, :] == 0)
-    base = base + jnp.where(corner[:, :, None, None], onsite[None, None, :, :], jnp.float32(0.0))
-    return jnp.pad(base, ((0, padded - bond), (0, padded - bond), (0, 0), (0, 0)))
-
-
 def iota(shape, dim):
     return lax.broadcasted_iota(jnp.int32, shape, dim)
 
@@ -39,27 +25,33 @@
     return jnp.dot(a, b, preferred_element_type=jnp.float32)
 
 
-def pack_kernel(cores, map_ref, held_ref, out_ref):
-    pool = held_ref.shape[0]
+def list_kernel(cores, pool, map_ref, list_ref):
     rows, tiles = map_ref.shape
     low = (lax.axis_index("env") * cores + lax.axis_index("col")) * pool
 
     def sector(t, carry):
         def step(j, count):
             slot = map_ref[t, j] - low
-            mine = (slot >= 0) & (slot < pool)
-            out_ref[t, count] = held_ref[jnp.where(mine, slot, 0)]
-            return count + mine.astype(jnp.int32)
-
-        lax.fori_loop(0, tiles, step, jnp.int32(0), unroll=8)
+            list_ref[t, count] = slot
+            return count + ((slot >= 0) & (slot < pool)).astype(jnp.int32)
+
+        lax.fori_loop(0, tiles, step, jnp.int32(0), unroll=16)
         return carry
 
     lax.fori_loop(0, rows, sector, jnp.int32(0))
 
 
+def quotient(value, divisor, limit):
+    for shift in range(8, 31):
+        factor = -(-(1 << shift) // divisor)
+        if limit * factor < 2**31 and (factor * divisor - (1 << shift)) * limit < 1 << shift:
+            return lax.shift_right_logical(value * factor, jnp.int32(shift))
+    return lax.div(value, jnp.int32(divisor))
+
+
 def comm_kernel(
-    sizes, pack_ref, left_ref, arrived_ref, other_ref,
-    z_send, z_recv, f_send, f_recv, x_send, x_recv, g_send, g_recv, own_sem,
+    sizes, list_ref, held_ref, left_ref, arrived_ref, other_ref, pool_ref, pack_ref,
+    z_send, z_recv, f_send, f_recv, x_send, x_recv, g_send, g_recv, own_sem, pool_sem,
 ):
     envs, planes, cores = sizes
     env, plane, core = lax.axis_index("env"), lax.axis_index("mpo"), lax.axis_index("col")
@@ -68,6 +60,8 @@
     part = left_ref.shape[2] // cores
     mate = lax.rem(core + 1, cores)
 
+    fill = pltpu.make_async_copy(held_ref, pool_ref, pool_sem)
+    fill.start()
     barrier = pltpu.get_barrier_semaphore()
     for d in range(1, envs):
         pl.semaphore_signal(
@@ -83,7 +77,7 @@
     def z_copy(d):
         target = lax.rem(env + d, envs)
         return pltpu.make_async_remote_copy(
-            src_ref=pack_ref.at[target, pl.ds(0, cap)],
+            src_ref=pack_ref.at[d],
             dst_ref=arrived_ref.at[env * cores + core],
             send_sem=z_send.at[d], recv_sem=z_recv.at[d],
             device_id={"env": target}, device_id_type=MESH,
@@ -93,7 +87,7 @@
         source = lax.rem(env - d + envs, envs)
         block = arrived_ref.at[source * cores + core]
         return pltpu.make_async_remote_copy(
-            src_ref=pack_ref.at[env, pl.ds(0, cap)] if d == 0 else block,
+            src_ref=pack_ref.at[0] if d == 0 else block,
             dst_ref=block,
             send_sem=f_send.at[d], recv_sem=f_recv.at[d],
             device_id={"col": mate}, device_id_type=MESH,
@@ -118,19 +112,32 @@
         )
 
     own = pltpu.make_async_copy(
-        pack_ref.at[env, pl.ds(0, cap)], arrived_ref.at[env * cores + core], own_sem
+        pack_ref.at[0], arrived_ref.at[env * cores + core], own_sem
     )
     z_order = list(range(envs - 1, 0, -1))
     x_order = [(d, w) for w in range(slab) for d in range(1, planes)]
-    for d in z_order:
-        z_copy(d).start()
     for d, w in x_order:
         x_copy(d, w).start()
-    own.start()
-    f_copy(0).start()
+    fill.wait()
+
+    def gather(d):
+        target = lax.rem(env + d, envs)
+
+        def step(p, carry):
+            slot = jnp.clip(list_ref[target, p], 0, pool_ref.shape[0] - 1)
+            pack_ref[d, p] = pool_ref[slot]
+            return carry
+
+        lax.fori_loop(0, cap, step, jnp.int32(0), unroll=8 if cap % 8 == 0 else 1)
+
+    for i, d in enumerate(z_order + [0]):
+        gather(d)
+        if i:
+            z_copy(z_order[i - 1]).start()
 
     waits = [("z", d, (i + 1) / len(z_order)) for i, d in enumerate(z_order)]
     waits += [("x", item, (i + 1) / len(x_order)) for i, item in enumerate(x_order)]
+    own_started = False
     for kind, item, _ in sorted(waits, key=lambda entry: entry[2]):
         if kind == "z":
             z_copy(item).wait_recv()
@@ -138,6 +145,10 @@
         else:
             x_copy(*item).wait_recv()
             g_copy(*item).start()
+        if not own_started:
+            own_started = True
+            own.start()
+            f_copy(0).start()
     own.wait()
     f_copy(0).wait()
     for d in z_order:
@@ -149,7 +160,7 @@
 
 
 def contract_kernel(
-    cores, pool, map_ref, kept_ref, arrived_ref, left_ref, other_ref, coupling_ref,
+    cores, pool, bond, map_ref, kept_ref, fields_ref, arrived_ref, left_ref, other_ref, coupling_ref,
     out_ref, count_ref, tiles_ref, own_ref, turned_ref, first_ref, second_ref,
 ):
     env, core = lax.axis_index("env"), lax.axis_index("col")
@@ -166,7 +177,7 @@
         count_ref[s] = 0
 
     def fetch(j, carry):
-        source = lax.div(map_ref[env, j], jnp.int32(pool))
+        source = quotient(map_ref[env, j], pool, pool * owners)
         rank = count_ref[source]
         count_ref[source] = rank + 1
         tiles_ref[pl.ds(pl.multiple_of(j * tile, tile), tile), :] = arrived_ref[
@@ -218,7 +229,20 @@
     diagonal = lax.rem(iota((tall, wide), 0), GROUP) == lax.rem(
         lax.div(iota((tall, wide), 1), padded), GROUP
     )
-    coupling = coupling_ref[...]
+    row, col = iota((pairs, states * padded), 0), iota((pairs, states * padded), 1)
+    state, slot = lax.div(col, padded), lax.rem(col, padded)
+    first_slot = lax.axis_index("mpo") * slab
+    turn = jnp.where(first_slot + slot >= slots, slots, 0)
+    corner = (
+        (first_slot + lax.div(row, states) == 0)
+        & (first_slot + slot - turn == bond - 1)
+        & (slot < slots)
+        & (lax.rem(row, states) == state)
+    )
+    onsite = fields_ref[0] * (0.5 - lax.div(state, 2).astype(jnp.float32)) + fields_ref[1] * (
+        0.5 - lax.rem(state, 2).astype(jnp.float32)
+    )
+    coupling = coupling_ref[...] + jnp.where(corner, onsite, 0.0)
     high = coupling.astype(BF)
     low = (coupling - high.astype(jnp.float32)).astype(BF)
     both = []
@@ -283,13 +307,13 @@
     anywhere = pl.BlockSpec(memory_space=pl.ANY)
     dma = pltpu.SemaphoreType.DMA
 
-    packed = pl.pallas_call(
-        functools.partial(pack_kernel, cores),
-        out_shape=jax.ShapeDtypeStruct((rows, cap + 1, tile, width), BF),
-        in_specs=[smem, vmem],
-        out_specs=vmem,
-        name="pack",
-    )(owner_map, held)
+    slot_list = pl.pallas_call(
+        functools.partial(list_kernel, cores, pool),
+        out_shape=jax.ShapeDtypeStruct((rows, cap + 1), jnp.int32),
+        in_specs=[smem],
+        out_specs=smem,
+        name="slots",
+    )(owner_map)
 
     arrived, other = pl.pallas_call(
         functools.partial(comm_kernel, (envs, planes, cores)),
@@ -297,18 +321,22 @@
             jax.ShapeDtypeStruct((envs * cores, cap, tile, width), BF),
             jax.ShapeDtypeStruct((slots - slab, width, width), BF),
         ],
-        in_specs=[anywhere, anywhere],
+        in_specs=[smem, anywhere, anywhere],
         out_specs=[anywhere, anywhere],
         scratch_shapes=[
+            pltpu.VMEM((pool, tile, width), BF),
+            pltpu.VMEM((envs, cap, tile, width), BF),
             dma((envs,)), dma((envs,)), dma((envs,)), dma((envs,)),
             dma((planes, slab)), dma((planes, slab)), dma((planes, slab)), dma((planes, slab)),
-            dma,
+            dma, dma,
         ],
         compiler_params=pltpu.CompilerParams(collective_id=0, has_side_effects=True),
         name="exchange",
-    )(packed, left_env)
-
-    couplings = build_couplings(mpo_tensor, mpo_mask, fields, slots)
+    )(slot_list, held, left_env)
+
+    bond = mpo_tensor.shape[0]
+    couplings = mpo_tensor * mpo_mask.astype(jnp.float32)[:, :, None, None]
+    couplings = jnp.pad(couplings, ((0, slots - bond), (0, slots - bond), (0, 0), (0, 0)))
     couplings = lax.dynamic_slice_in_dim(couplings, plane * slab, slab, 1)
     couplings = jnp.concatenate([couplings, couplings], axis=0)
     couplings = lax.dynamic_slice_in_dim(couplings, plane * slab, slots, 0)
@@ -317,9 +345,9 @@
 
     chunk_rows = 64 * padded
     result = pl.pallas_call(
-        functools.partial(contract_kernel, cores, pool),
+        functools.partial(contract_kernel, cores, pool, bond),
         out_shape=jax.ShapeDtypeStruct((slab, share, width), jnp.float32),
-        in_specs=[smem, smem, vmem, vmem, vmem, vmem],
+        in_specs=[smem, smem, smem, vmem, vmem, vmem, vmem],
         out_specs=vmem,
         scratch_shapes=[
             pltpu.SMEM((envs * cores,), jnp.int32),
@@ -331,7 +359,7 @@
         ],
         compiler_params=pltpu.CompilerParams(vmem_limit_bytes=48 * 1024 * 1024),
         name="contract",
-    )(owner_map, kept, arrived, left_env, other, couplings)
+    )(owner_map, kept, fields, arrived, left_env, other, couplings)
     return jnp.swapaxes(result, 1, 2)[:, None]
 
 

time: 71.5 us -> 67.5 us (0.944)
  other arithmetic: 2.41 us -> 0.85 us
  local copies, waits for them, and re-layouts: 3.54 us -> 2.14 us
  Pallas kernels: 64.4 us -> 63.4 us
    pallas_call x2, Pallas kernels: 29.6 us -> 27.5 us  [the longest x1 21.5 us: on_device(): pl.pallas_call(functools.partial(contract_kernel, cores, pool, bond), out...]
    add x2 -> x0, other arithmetic: 1.42 us -> none  [the longest x1 1.34 us: build_couplings(): onsite = jnp.diag(fields[0] * spin_first + fields[1] * spin_second)]
    slice x1 -> x0, local copies, waits for them, and re-layouts: 1.39 us -> none  [build_couplings(): onsite = jnp.diag(fields[0] * spin_first + fields[1] * spin_second)]
    pallas_call x1, Pallas kernels: 34.9 us -> 35.8 us  [on_device(): pl.pallas_call(functools.partial(comm_kernel, (envs, planes, cores)), out...]
    unnamed x9 -> x11, local copies, waits for them, and re-layouts: 1.81 us -> 1.82 us
where the time goes in v2:
time: 67.5 us; the launch traced here: 67.3 us
  Pallas kernels  63.4 us (94%)
  local copies, waits for them, and re-layouts  2.14 us (3%)
  between operations  0.89 us (1%)
  other arithmetic  0.85 us (1%)
    pallas_call x1, Pallas kernels, on_device(): pl.pallas_call(functools.partial(comm_kernel, (envs, planes, cores)), out...  35.8 us
    pallas_call x1, Pallas kernels, on_device(): pl.pallas_call(functools.partial(contract_kernel, cores, pool, bond), out...  21.5 us
    pallas_call x1, Pallas kernels, on_device(): pl.pallas_call(functools.partial(list_kernel, cores, pool), out_shape=jax...  6.03 us
    unnamed x11, local copies, waits for them, and re-layouts  1.82 us

profile of v2, /device:TPU:0, one launch (start us, length us, event | category | flops | bytes accessed | tf_op | source)
XLA Modules:
  0.0 67.3 jit_solution(5300983613080291342)
XLA Ops:
  0.0 0.0 copy-start
  0.0 0.0 copy-start.1
  0.0 0.0 copy-start.3
  0.0 0.0 copy-start.4
  0.8 6.0 %slots.1.list_ref = s32[4,49]{1,0:T(4,128)} custom-call(s32[4,192]{1,0:T(4,128)} %map_ref.3), custom_call_target="tpu_custom_call" | custom-call | tf_op jit(solution)/shard_map/slots/pallas_call | solution.py:310
  6.8 0.7 %convert_element_type.5 = f32[14,14]{1,0:T(8,128)S(1)} convert(s32[14,14]{1,0:T(8,128)} %param.12) | non-fusion elementwise | flops 196 | bytes 1568 | tf_op jit(solution)/shard_map/convert_element_type | solution.py:338
  7.5 0.1 copy.10
  7.7 0.0 copy-done
  7.7 0.1 constant_dynamic-slice_fusion
  7.8 0.2 copy.13
  8.0 0.1 dynamic-slice_maximum_fusion
  8.2 0.1 reshape.4.coupling_ref
  8.3 35.8 %exchange.1 = (bf16[8,48,8,384]{3,2,1,0:T(8,128)(2,1)}, bf16[7,384,384]{2,1,0:T(8,128)(2,1)}) custom-call(s32[4,49]{1,0:T(4,128)} %slots.1.list_ref, bf16[192,8,384]{2,1,0:T(8,128)(2,1)} %held_ref.1, bf16[7,1,384,384]{3,2,1,0:T(8,128)(2,1)} %left_ref.3), custom_call_target="tpu_custom_call" | custom-call | tf_op jit(solution)/shard_map/exchange/pallas_call | solution.py:318
  44.1 0.0 copy-done.1
  44.1 0.0 copy-done.3
  44.2 0.0 copy-done.4
  44.2 0.0 copy-start.2
  44.2 1.6 %copy-done.2 = bf16[7,384,384]{2,1,0:T(8,128)(2,1)S(1)} copy-done((bf16[7,384,384]{2,1,0:T(8,128)(2,1)S(1)}, bf16[7,384,384]{2,1,0:T(8,128)(2,1)}, u32[]{:S(2)}) %copy-start.2) | copy-done | bytes 2064408
  45.7 21.5 %contract.1 = f32[7,192,384]{2,1,0:T(8,128)} custom-call(s32[4,192]{1,0:T(4,128)S(1)} %copy-done.3, s32[1]{0:T(128)S(6)} %copy.14.kept_ref, f32[2]{0:T(128)S(1)} %copy-done.4, bf16[8,48,8,384]{3,2,1,0:T(8,128)(2,1)} %get-tuple-element.7.arrived_ref, bf16[7,1,384,384]{3,2,1,0:T(8,128)(2,1)S(1)} %copy-done.1, bf16[7,384,384]{2,1,0:T(8,128)(2,1)S(1)} %copy-done.2, ...), custom_call_target="tpu_custom_call" | custom-call | tf_op jit(solution)/shard_map/contract/pallas_call | solution.py:347
  (3 shorter events, 0.0 us)
Async XLA Ops:
  0.0 7.7 %copy-start = (f32[14,14,4,4]{1,3,2,0:T(4,128)S(1)}, f32[14,14,4,4]{1,3,2,0:T(4,128)}, u32[]{:S(2)}) copy-start(f32[14,14,4,4]{1,3,2,0:T(4,128)} %param.11) | copy-start | bytes 37636
  0.0 44.1 %copy-start.1 = (bf16[7,1,384,384]{3,2,1,0:T(8,128)(2,1)S(1)}, bf16[7,1,384,384]{3,2,1,0:T(8,128)(2,1)}, u32[]{:S(2)}) copy-start(bf16[7,1,384,384]{3,2,1,0:T(8,128)(2,1)} %left_ref.3) | copy-start | bytes 6193156
  0.0 44.1 %copy-start.3 = (s32[4,192]{1,0:T(4,128)S(1)}, s32[4,192]{1,0:T(4,128)}, u32[]{:S(2)}) copy-start(s32[4,192]{1,0:T(4,128)} %map_ref.3) | copy-start | bytes 9220
  0.0 44.1 %copy-start.4 = (f32[2]{0:T(128)S(1)}, f32[2]{0:T(128)}, u32[]{:S(2)}) copy-start(f32[2]{0:T(128)} %fields_ref.1) | copy-start | bytes 28
  44.2 1.6 %copy-start.2 = (bf16[7,384,384]{2,1,0:T(8,128)(2,1)S(1)}, bf16[7,384,384]{2,1,0:T(8,128)(2,1)}, u32[]{:S(2)}) copy-start(bf16[7,384,384]{2,1,0:T(8,128)(2,1)} %get-tuple-element.8.other_ref) | copy-start | bytes 6193156

commit v3 on v2

--- a/solution.py
+++ b/solution.py
@@ -28,14 +28,20 @@
 def list_kernel(cores, pool, map_ref, list_ref):
     rows, tiles = map_ref.shape
     low = (lax.axis_index("env") * cores + lax.axis_index("col")) * pool
+    batch = 16 if tiles % 16 == 0 else 1
 
     def sector(t, carry):
-        def step(j, count):
-            slot = map_ref[t, j] - low
-            list_ref[t, count] = slot
-            return count + ((slot >= 0) & (slot < pool)).astype(jnp.int32)
-
-        lax.fori_loop(0, tiles, step, jnp.int32(0), unroll=16)
+        def step(b, count):
+            found = [map_ref[t, b * batch + i] - low for i in range(batch)]
+            places = [count]
+            for slot in found:
+                mine = (slot >= 0) & (slot < pool)
+                places.append(places[-1] + mine.astype(jnp.int32))
+            for slot, place in zip(found, places):
+                list_ref[t, place] = slot
+            return places[-1]
+
+        lax.fori_loop(0, tiles // batch, step, jnp.int32(0))
         return carry
 
     lax.fori_loop(0, rows, sector, jnp.int32(0))
@@ -160,8 +166,8 @@
 
 
 def contract_kernel(
-    cores, pool, bond, map_ref, kept_ref, fields_ref, arrived_ref, left_ref, other_ref, coupling_ref,
-    out_ref, count_ref, tiles_ref, own_ref, turned_ref, first_ref, second_ref,
+    cores, pool, bond, map_ref, kept_ref, fields_ref, arrived_ref, near_ref, far_ref, coupling_ref,
+    out_ref, left_ref, other_ref, load_sem, count_ref, tiles_ref, own_ref, turned_ref, first_ref, second_ref,
 ):
     env, core = lax.axis_index("env"), lax.axis_index("col")
     owners, cap, tile, width = arrived_ref.shape
@@ -173,19 +179,32 @@
     share = width // cores
     lanes = own_ref.shape[2]
 
+    loads = [
+        pltpu.make_async_copy(near_ref, left_ref, load_sem.at[0]),
+        pltpu.make_async_copy(far_ref, other_ref, load_sem.at[1]),
+    ]
+    for load in loads:
+        load.start()
+
     for s in range(owners):
         count_ref[s] = 0
 
-    def fetch(j, carry):
-        source = quotient(map_ref[env, j], pool, pool * owners)
-        rank = count_ref[source]
-        count_ref[source] = rank + 1
-        tiles_ref[pl.ds(pl.multiple_of(j * tile, tile), tile), :] = arrived_ref[
-            source, rank
-        ].astype(jnp.float32)
+    batch = 16 if tiles % 16 == 0 else 1
+
+    def fetch(b, carry):
+        sources = [
+            quotient(map_ref[env, b * batch + i], pool, pool * owners) for i in range(batch)
+        ]
+        ranks = []
+        for source in sources:
+            ranks.append(count_ref[source])
+            count_ref[source] = ranks[-1] + 1
+        for i in range(batch):
+            at = pl.multiple_of((b * batch + i) * tile, tile)
+            tiles_ref[pl.ds(at, tile), :] = arrived_ref[sources[i], ranks[i]].astype(jnp.float32)
         return carry
 
-    lax.fori_loop(0, tiles, fetch, jnp.int32(0), unroll=8)
+    lax.fori_loop(0, tiles // batch, fetch, jnp.int32(0))
 
     kept = kept_ref[0]
     blocks = [
@@ -281,6 +300,8 @@
                 second_ref[v, pl.ds(at, unit), :] = mixed[v * unit : (v + 1) * unit]
         return carry
 
+    for load in loads:
+        load.wait()
     lax.fori_loop(0, width // rows_chunk, chunk_step, jnp.int32(0))
 
     def close(v, carry):
@@ -347,9 +368,12 @@
     result = pl.pallas_call(
         functools.partial(contract_kernel, cores, pool, bond),
         out_shape=jax.ShapeDtypeStruct((slab, share, width), jnp.float32),
-        in_specs=[smem, smem, smem, vmem, vmem, vmem, vmem],
+        in_specs=[smem, smem, smem, vmem, anywhere, anywhere, vmem],
         out_specs=vmem,
         scratch_shapes=[
+            pltpu.VMEM(left_env.shape, BF),
+            pltpu.VMEM((slots - slab, width, width), BF),
+            dma((2,)),
             pltpu.SMEM((envs * cores,), jnp.int32),
             pltpu.VMEM((tiles * tile, width), jnp.float32),
             pltpu.VMEM((states, width, lanes), BF),
@@ -357,7 +381,7 @@
             pltpu.VMEM((states, chunk_rows, lanes), BF),
             pltpu.VMEM((slab, tiles * tile, lanes), BF),
         ],
-        compiler_params=pltpu.CompilerParams(vmem_limit_bytes=48 * 1024 * 1024),
+        compiler_params=pltpu.CompilerParams(vmem_limit_bytes=62 * 1024 * 1024),
         name="contract",
     )(owner_map, kept, fields, arrived, left_env, other, couplings)
     return jnp.swapaxes(result, 1, 2)[:, None]

time: 67.5 us -> 66.9 us (level)
  local copies, waits for them, and re-layouts: 2.14 us -> 1.16 us
    unnamed x11 -> x3, local copies, waits for them, and re-layouts: 1.82 us -> 0.23 us
    pallas_call x1, Pallas kernels: 6.03 us -> 6.72 us  [on_device(): pl.pallas_call(functools.partial(list_kernel, cores, pool), out_shape=jax...]
where the time goes in v3:
time: 66.9 us; the launch traced here: 66.6 us
  Pallas kernels  63.9 us (96%)
  local copies, waits for them, and re-layouts  1.16 us (2%)
  other arithmetic  0.85 us (1%)
  between operations  0.74 us (1%)
    pallas_call x1, Pallas kernels, on_device(): pl.pallas_call(functools.partial(comm_kernel, (envs, planes, cores)), out...  35.8 us
    pallas_call x1, Pallas kernels, on_device(): pl.pallas_call(functools.partial(contract_kernel, cores, pool, bond), out...  21.4 us
    pallas_call x1, Pallas kernels, on_device(): pl.pallas_call(functools.partial(list_kernel, cores, pool), out_shape=jax...  6.72 us

profile of v3, /device:TPU:0, one launch (start us, length us, event | category | flops | bytes accessed | tf_op | source)
XLA Modules:
  0.0 66.6 jit_solution(15272800231954036505)
XLA Ops:
  0.0 0.0 copy-start
  0.7 6.7 %slots.1.list_ref = s32[4,49]{1,0:T(4,128)} custom-call(s32[4,192]{1,0:T(4,128)} %map_ref.3), custom_call_target="tpu_custom_call" | custom-call | tf_op jit(solution)/shard_map/slots/pallas_call | solution.py:331
  7.4 0.7 %convert_element_type.5 = f32[14,14]{1,0:T(8,128)S(1)} convert(s32[14,14]{1,0:T(8,128)} %param.12) | non-fusion elementwise | flops 196 | bytes 1568 | tf_op jit(solution)/shard_map/convert_element_type | solution.py:359
  8.1 0.1 copy.10
  8.2 0.0 copy-done
  8.2 0.1 constant_dynamic-slice_fusion
  8.4 0.2 copy.13
  8.6 0.1 dynamic-slice_maximum_fusion
  8.8 0.7 %reshape.4.coupling_ref = f32[28,64]{1,0:T(8,128)} reshape(f32[7,4,4,16]{3,2,1,0:T(4,128)S(1)} %pad_bitcast_fusion) | data formatting | bytes 14336 | tf_op jit(solution)/shard_map/reshape | solution.py:365
  9.5 35.8 %exchange.1 = (bf16[8,48,8,384]{3,2,1,0:T(8,128)(2,1)}, bf16[7,384,384]{2,1,0:T(8,128)(2,1)}) custom-call(s32[4,49]{1,0:T(4,128)} %slots.1.list_ref, bf16[192,8,384]{2,1,0:T(8,128)(2,1)} %held_ref.1, bf16[7,1,384,384]{3,2,1,0:T(8,128)(2,1)} %near_ref.1), custom_call_target="tpu_custom_call" | custom-call | tf_op jit(solution)/shard_map/exchange/pallas_call | solution.py:339
  45.3 21.4 %contract.1 = f32[7,192,384]{2,1,0:T(8,128)} custom-call(s32[4,192]{1,0:T(4,128)} %map_ref.3, s32[1]{0:T(128)S(6)} %copy.14.kept_ref, f32[2]{0:T(128)} %fields_ref.1, bf16[8,48,8,384]{3,2,1,0:T(8,128)(2,1)} %get-tuple-element.7.arrived_ref, bf16[7,1,384,384]{3,2,1,0:T(8,128)(2,1)} %near_ref.1, bf16[7,384,384]{2,1,0:T(8,128)(2,1)} %get-tuple-element.8.far_ref, ...), custom_call_target="tpu_custom_call" | custom-call | tf_op jit(solution)/shard_map/contract/pallas_call | solution.py:368
  (3 shorter events, 0.0 us)
Async XLA Ops:
  0.0 8.2 %copy-start = (f32[14,14,4,4]{1,3,2,0:T(4,128)S(1)}, f32[14,14,4,4]{1,3,2,0:T(4,128)}, u32[]{:S(2)}) copy-start(f32[14,14,4,4]{1,3,2,0:T(4,128)} %param.11) | copy-start | bytes 37636

commit v4 on v3

--- a/solution.py
+++ b/solution.py
@@ -35,8 +35,8 @@
             found = [map_ref[t, b * batch + i] - low for i in range(batch)]
             places = [count]
             for slot in found:
-                mine = (slot >= 0) & (slot < pool)
-                places.append(places[-1] + mine.astype(jnp.int32))
+                mine = lax.shift_right_logical(~slot & (slot - pool), jnp.int32(31))
+                places.append(places[-1] + mine)
             for slot, place in zip(found, places):
                 list_ref[t, place] = slot
             return places[-1]

time: 66.9 us -> 66.8 us (level)
  no operation moved by 1% of the time
where the time goes in v4:
time: 66.8 us; the launch traced here: 66.5 us
  Pallas kernels  63.7 us (95%)
  local copies, waits for them, and re-layouts  1.16 us (2%)
  other arithmetic  0.85 us (1%)
  between operations  0.74 us (1%)
    pallas_call x1, Pallas kernels, on_device(): pl.pallas_call(functools.partial(comm_kernel, (envs, planes, cores)), out...  35.8 us
    pallas_call x1, Pallas kernels, on_device(): pl.pallas_call(functools.partial(contract_kernel, cores, pool, bond), out...  21.4 us
    pallas_call x1, Pallas kernels, on_device(): pl.pallas_call(functools.partial(list_kernel, cores, pool), out_shape=jax...  6.55 us

profile of v4, /device:TPU:0, one launch (start us, length us, event | category | flops | bytes accessed | tf_op | source)
XLA Modules:
  0.0 66.5 jit_solution(3558978513942497665)
XLA Ops:
  0.0 0.0 copy-start
  0.7 6.5 %slots.1.list_ref = s32[4,49]{1,0:T(4,128)} custom-call(s32[4,192]{1,0:T(4,128)} %map_ref.3), custom_call_target="tpu_custom_call" | custom-call | tf_op jit(solution)/shard_map/slots/pallas_call | solution.py:331
  7.2 0.7 %convert_element_type.5 = f32[14,14]{1,0:T(8,128)S(1)} convert(s32[14,14]{1,0:T(8,128)} %param.12) | non-fusion elementwise | flops 196 | bytes 1568 | tf_op jit(solution)/shard_map/convert_element_type | solution.py:359
  7.9 0.1 copy.10
  8.1 0.0 copy-done
  8.1 0.1 constant_dynamic-slice_fusion
  8.2 0.2 copy.13
  8.4 0.1 dynamic-slice_maximum_fusion
  8.6 0.7 %reshape.4.coupling_ref = f32[28,64]{1,0:T(8,128)} reshape(f32[7,4,4,16]{3,2,1,0:T(4,128)S(1)} %pad_bitcast_fusion) | data formatting | bytes 14336 | tf_op jit(solution)/shard_map/reshape | solution.py:365
  9.3 35.8 %exchange.1 = (bf16[8,48,8,384]{3,2,1,0:T(8,128)(2,1)}, bf16[7,384,384]{2,1,0:T(8,128)(2,1)}) custom-call(s32[4,49]{1,0:T(4,128)} %slots.1.list_ref, bf16[192,8,384]{2,1,0:T(8,128)(2,1)} %held_ref.1, bf16[7,1,384,384]{3,2,1,0:T(8,128)(2,1)} %near_ref.1), custom_call_target="tpu_custom_call" | custom-call | tf_op jit(solution)/shard_map/exchange/pallas_call | solution.py:339
  45.1 21.4 %contract.1 = f32[7,192,384]{2,1,0:T(8,128)} custom-call(s32[4,192]{1,0:T(4,128)} %map_ref.3, s32[1]{0:T(128)S(6)} %copy.14.kept_ref, f32[2]{0:T(128)} %fields_ref.1, bf16[8,48,8,384]{3,2,1,0:T(8,128)(2,1)} %get-tuple-element.7.arrived_ref, bf16[7,1,384,384]{3,2,1,0:T(8,128)(2,1)} %near_ref.1, bf16[7,384,384]{2,1,0:T(8,128)(2,1)} %get-tuple-element.8.far_ref, ...), custom_call_target="tpu_custom_call" | custom-call | tf_op jit(solution)/shard_map/contract/pallas_call | solution.py:368
  (3 shorter events, 0.0 us)
Async XLA Ops:
  0.0 8.1 %copy-start = (f32[14,14,4,4]{1,3,2,0:T(4,128)S(1)}, f32[14,14,4,4]{1,3,2,0:T(4,128)}, u32[]{:S(2)}) copy-start(f32[14,14,4,4]{1,3,2,0:T(4,128)} %param.11) | copy-start | bytes 37636
